TPU v7x, 32 devices: a whole 2x2x4 slice. The times are simulated.
32 devices in a mesh: ea: 8 (over z, y), ba: 4 (over x, core).
Axes of the slice: x: 2, y: 2, z: 4, core: 2. Of those that a mesh axis runs over, the one named last changes fastest.
Arguments:
- entities: float32 [4096, 200], P('ea'), may hold values from -1.5 to 1.5
- entity_history: float32 [4096], P('ea'), may hold values from 0.001 to 0.1
- relations: float32 [256, 200], replicated, may hold values from -6 to 6
- relation_history: float32 [256], replicated, may hold values from 0.001 to 0.1
- edge_ends: int32 [8192, 2], P(('ba', 'ea')), may hold values from 0 to 4095, as said below
- edge_relations: int32 [8192], P(('ba', 'ea')), may hold values from 0 to 255
- negatives: int32 [8192], P(('ba', 'ea')), may hold values from 0 to 4095, as said below
Outputs:
- entity_step: float32 [4096, 200], P('ea')
- entity_squares: float32 [4096], P('ea')
- relation_step: float32 [256, 200], replicated
- relation_squares: float32 [256], replicated
- mean_loss: float32 [1], replicated
Inputs may be any that keep to these rules, and one draw needn't show every extreme that they name: `edge_ends`: every entry is an entity id. In each aligned block of 256 edges at most 48 heads have the same owner shard (id // 512), and some shard has exactly 48; the same holds for the tails. Every entry is an entity id. In each run of 256 consecutive negatives at most 48 have the same owner shard (id // 512), and some shard has exactly 48. `edge_relations`: every entry is a relation id.
All inputs are finite; a program needn't handle non-finite values.
Results may differ from a plain program's by a relative error of at most 0.0003.
Values sent between devices are 32-bit elements.
A program may use at most 64 MiB of HBM per device.

v0:
```python
import jax
import jax.numpy as jnp
from jax import lax
from jax.sharding import PartitionSpec as P

learn_rate = 0.1
adagrad_eps = 1e-10
highest = lax.Precision.HIGHEST


def halves(vectors):
    half_width = vectors.shape[-1] // 2
    return (vectors[..., :half_width], vectors[..., half_width:])


def complex_times(former, latter):
    former_real, former_imag = halves(former)
    latter_real, latter_imag = halves(latter)
    return jnp.concatenate(
        [
            former_real * latter_real - former_imag * latter_imag,
            former_real * latter_imag + former_imag * latter_real,
        ],
        axis=-1,
    )


def conjugate(vectors):
    real_part, imag_part = halves(vectors)
    return jnp.concatenate([real_part, -imag_part], axis=-1)


def adagrad_step(slope_vector, history):
    squares = history + jnp.mean(slope_vector * slope_vector, axis=1)
    return (-learn_rate * slope_vector / (jnp.sqrt(squares)[:, None] + adagrad_eps), squares)


def bucket_slots(node_labels, shard_rows, peer_count, room_limit):
    owners = node_labels // shard_rows
    local_rows = node_labels - owners * shard_rows
    onehot = (owners[:, None] == jnp.arange(peer_count, dtype=jnp.int32)[None, :]).astype(jnp.int32)
    earlier = jnp.cumsum(onehot, axis=0) - onehot
    slot_positions = owners * room_limit + jnp.sum(earlier * onehot, axis=1)
    request = jnp.full((peer_count * room_limit,), -1, jnp.int32).at[slot_positions].set(local_rows)
    return (slot_positions, request.reshape(peer_count, room_limit))


def serve_rows(table, demanded_lookups):
    picked = jnp.take(table, jnp.maximum(demanded_lookups, 0), axis=0)
    return jnp.where((demanded_lookups >= 0)[..., None], picked, 0.0)


def outgoing_rows(slope_vector, slot_positions, peer_count, room_limit):
    buffer_rows = (
        jnp.zeros((peer_count * room_limit, slope_vector.shape[1]), jnp.float32)
        .at[slot_positions]
        .set(slope_vector)
    )
    return buffer_rows.reshape(peer_count, room_limit, slope_vector.shape[1])


def absorb(dense_grad, demanded_lookups, incoming):
    flat_rows = jnp.maximum(demanded_lookups, 0).reshape(-1)
    return dense_grad.at[flat_rows].add(incoming.reshape(-1, incoming.shape[-1]))


def matmul(former, latter):
    return jnp.dot(former, latter, precision=highest, preferred_element_type=jnp.float32)


def spread_back(weights, probe_rows):
    return lax.dot_general(
        weights,
        probe_rows,
        (((0,), (0,)), ((), ())),
        precision=highest,
        preferred_element_type=jnp.float32,
    )


def side_terms(probe_rows, positive, candidates):
    scores = lax.dot_general(
        probe_rows,
        candidates,
        (((1,), (1,)), ((), ())),
        precision=highest,
        preferred_element_type=jnp.float32,
    )
    own_edge = lax.broadcasted_iota(jnp.int32, scores.shape, 1) == lax.broadcasted_iota(
        jnp.int32, scores.shape, 0
    )
    scores = jnp.where(own_edge, -jnp.inf, scores)
    peak = jnp.maximum(jnp.max(scores, axis=1), positive)
    lifted = jnp.exp(scores - peak[:, None])
    struck = jnp.exp(positive - peak)
    normal = struck + jnp.sum(lifted, axis=1)
    loss_sum = jnp.sum(jnp.log(normal) + peak - positive)
    return (loss_sum, lifted / normal[:, None], struck / normal)


def on_device(
    entities, entity_history, relations, relation_history, edge_ends, edge_relations, negatives
):
    peer_count = lax.axis_size("ea")
    shard_rows = entities.shape[0]
    row_width = entities.shape[1]
    edge_count = edge_ends.shape[0]
    negative_count = negatives.shape[0]
    edge_share = edge_count // peer_count
    link_room = edge_share + max(1, edge_share // 2)
    negative_share = negative_count // peer_count
    contrast_room = negative_share + max(1, negative_share // 2)
    desired_items = (edge_ends[:, 0], edge_ends[:, 1], negatives)
    room_limits = (link_room, link_room, contrast_room)
    joint_capacity = sum(room_limits)
    joint_places, joint_request = bucket_slots(
        jnp.concatenate(desired_items), shard_rows, peer_count, joint_capacity
    )
    joint_asked = lax.all_to_all(joint_request, "ea", split_axis=0, concat_axis=0, tiled=True)
    joint_answer = lax.all_to_all(
        serve_rows(entities, joint_asked), "ea", split_axis=0, concat_axis=0, tiled=True
    )
    fetched = joint_answer.reshape(-1, row_width)[joint_places]
    head_rows = fetched[:edge_count]
    tail_rows = fetched[edge_count : 2 * edge_count]
    negative_rows = fetched[2 * edge_count :]
    related = jnp.take(relations, edge_relations, axis=0)
    tail_query = complex_times(head_rows, related)
    head_probe = complex_times(conjugate(related), tail_rows)
    positive = jnp.sum(tail_query * tail_rows, axis=1)
    tail_cands = jnp.concatenate([tail_rows, negative_rows], axis=0)
    head_cands = jnp.concatenate([head_rows, negative_rows], axis=0)
    tail_loss, tail_weight, tail_struck = side_terms(tail_query, positive, tail_cands)
    head_loss, head_weight, head_struck = side_terms(head_probe, positive, head_cands)
    gain = tail_struck + head_struck - 2.0
    tail_back = matmul(tail_weight, tail_cands) + gain[:, None] * tail_rows
    head_back = matmul(head_weight, head_cands)
    tail_spread = spread_back(tail_weight, tail_query)
    head_spread = spread_back(head_weight, head_probe)
    head_grad = complex_times(tail_back, conjugate(related)) + head_spread[:edge_count]
    tail_grad = (
        gain[:, None] * tail_query + complex_times(head_back, related) + tail_spread[:edge_count]
    )
    negative_grad = tail_spread[edge_count:] + head_spread[edge_count:]
    relation_rows = complex_times(tail_back, conjugate(head_rows)) + complex_times(
        conjugate(head_back), tail_rows
    )
    relation_local = jax.ops.segment_sum(
        relation_rows, edge_relations, num_segments=relations.shape[0]
    )
    loss_local = tail_loss + head_loss
    dense_grad = jnp.zeros((shard_rows, row_width), jnp.float32)
    joint_grad = jnp.concatenate([head_grad, tail_grad, negative_grad], axis=0)
    incoming = lax.all_to_all(
        outgoing_rows(joint_grad, joint_places, peer_count, joint_capacity),
        "ea",
        split_axis=0,
        concat_axis=0,
        tiled=True,
    )
    dense_grad = absorb(dense_grad, joint_asked, incoming)
    relation_sum, loss_sum = lax.psum((relation_local, loss_local), ("ea", "ba"))
    relation_step, relation_squares = adagrad_step(relation_sum, relation_history)
    mean_loss = (loss_sum / (2.0 * edge_count * peer_count * lax.axis_size("ba"))).reshape(1)
    summed = lax.psum(dense_grad, "ba")
    entity_step, entity_squares = adagrad_step(summed, entity_history)
    return (entity_step, entity_squares, relation_step, relation_squares, mean_loss)


def solution(mesh):
    placed = (
        P("ea", None),
        P("ea"),
        P(),
        P(),
        P(("ba", "ea"), None),
        P(("ba", "ea")),
        P(("ba", "ea")),
    )
    return jax.shard_map(
        on_device,
        mesh=mesh,
        in_specs=placed,
        out_specs=(P("ea", None), P("ea"), P(), P(), P()),
        check_vma=False,
    )
```

profile of v0, /device:TPU:0, one launch (start us, length us, event | category | flops | bytes accessed | tf_op | source)
XLA Modules:
  0.0 283.6 jit_solution(15245476762388330828)
XLA Ops:
  8.0 0.8 fusion.40
  9.5 1.7 reduce-window.6
  11.7 0.7 multiply_subtract_fusion.6
  12.4 0.7 fusion.25
  13.2 3.4 %scatter_custom_fusion = s32[1152]{0:T(1024)S(1)} fusion(s32[768]{0:T(1024)S(1)} %fusion.25, s32[768]{0:T(1024)S(1)} %get-tuple-element.59, s32[]{:T(128)} %constant.34.clone.1), kind=kCustom, calls=%fused_computation.89 | custom fusion | bytes 4612 | tf_op jit(solution)/shard_map/scatter | solution.py:44
  17.2 7.3 %all-to-all-start = ((s32[8,1,144]{2,1,0:T(1,128)}), s32[8,1,144]{2,1,0:T(1,128)S(1)}, u32[]{:S(2)}, u32[]{:S(2)}) async-start(s32[8,1,144]{2,1,0:T(1,128)} %all_to_all.12), calls=%async_computation | async-start | bytes 16384 | tf_op jit(solution)/shard_map/all_to_all | solution.py:119
  24.5 1.2 copy.54
  25.8 5.3 %all-to-all-done = s32[8,1,144]{2,1,0:T(1,128)S(1)} async-done(((s32[8,1,144]{2,1,0:T(1,128)}), s32[8,1,144]{2,1,0:T(1,128)S(1)}, u32[]{:S(2)}, u32[]{:S(2)}) %all-to-all-start) | async-done | bytes 4640 | tf_op jit(solution)/shard_map/all_to_all | solution.py:119
  31.2 3.3 %gather_fusion = f32[1152,200]{1,0:T(8,128)S(1)} fusion(f32[512,200]{1,0:T(8,128)S(1)} %copy.54, s32[2048]{0:T(1024)S(1)} %pad_clamp_fusion), kind=kCustom, calls=%fused_computation | custom fusion | bytes 1847808 | tf_op jit(solution)/shard_map/jit(_take)/gather | solution.py:49
  34.5 1.3 select_select_fusion
  35.8 3.9 %all-to-all-start.1 = ((f32[8,144,200]{2,1,0:T(8,128)}), f32[8,144,200]{2,1,0:T(8,128)S(1)}, u32[]{:S(2)}, u32[]{:S(2)}) async-start(f32[8,144,200]{2,1,0:T(8,128)} %select_select_fusion), calls=%async_computation.1 | async-start | bytes 2359296 | tf_op jit(solution)/shard_map/all_to_all | solution.py:120
  39.9 1.0 gather_fusion.2
  41.0 25.8 %all-to-all-done.1 = f32[8,144,200]{2,1,0:T(8,128)S(1)} async-done(((f32[8,144,200]{2,1,0:T(8,128)}), f32[8,144,200]{2,1,0:T(8,128)S(1)}, u32[]{:S(2)}, u32[]{:S(2)}) %all-to-all-start.1) | async-done | bytes 921632 | tf_op jit(solution)/shard_map/all_to_all | solution.py:120
  66.9 2.1 gather_fusion.1
  69.8 1.2 fusion.43
  71.0 1.2 fusion.42
  73.1 1.1 fusion.8
  74.3 0.7 fusion.11
  75.0 0.7 fusion.14
  75.7 1.1 convolution_add_fusion
  77.4 6.6 %scatter_custom_fusion.1 = f32[1152,200]{1,0:T(8,128)} fusion(s32[768]{0:T(1024)S(1)} %fusion.25, f32[768,200]{1,0:T(8,128)S(1)} %copy.62, f32[]{:T(128)} %constant.33.clone.1), kind=kCustom, calls=%fused_computation.12 | custom fusion | bytes 921604 | tf_op jit(solution)/shard_map/scatter | solution.py:57
  84.0 3.6 %all-to-all-start.2 = ((f32[8,144,200]{2,1,0:T(8,128)}), f32[8,144,200]{2,1,0:T(8,128)S(1)}, u32[]{:S(2)}, u32[]{:S(2)}) async-start(f32[8,144,200]{2,1,0:T(8,128)} %bitcast.10), calls=%async_computation.2 | async-start | bytes 2359296 | tf_op jit(solution)/shard_map/all_to_all | solution.py:154
  88.0 2.6 scatter_custom_fusion.3
  92.0 45.4 %psum.23 = f32[]{:T(128)} all-reduce(f32[]{:T(128)S(6)} %add.183), channel_id=1, replica_groups=mesh['ea'=8,'ba'=4] {'ea','ba'}, use_global_device_ids=true, to_apply=%region_18.19 | all-reduce | flops 1 | bytes 8 | tf_op jit(solution)/shard_map/psum | solution.py:162
  138.1 89.3 %all-reduce.5.cloned.1.call-done = f32[256,200]{1,0:T(8,128)} async-done(((f32[256,200]{1,0:T(8,128)}), f32[256,200]{1,0:T(8,128)}) %all-reduce.5.cloned.1.call-update) | async-done | bytes 204816 | tf_op jit(solution)/shard_map/psum | solution.py:162
  227.3 1.1 multiply_reduce_fusion.1
  229.0 9.3 %scatter_custom_fusion.2 = f32[512,200]{1,0:T(8,128)} fusion(s32[1152]{0:T(1024)S(1)} %reshape.425, f32[1152,200]{1,0:T(8,128)S(1)} %bitcast.44, f32[]{:T(128)} %constant.33.clone.1), kind=kCustom, calls=%fused_computation.29 | custom fusion | flops 230400 | bytes 409604 | tf_op jit(solution)/shard_map/scatter-add | solution.py:64
  238.5 0.8 copy.65
  239.3 31.8 %all-reduce.3.cloned.1.call-done = f32[512,200]{1,0:T(8,128)} async-done(((f32[512,200]{1,0:T(8,128)}), f32[512,200]{1,0:T(8,128)}) %all-reduce.3.cloned.1.call-update) | async-done | bytes 409616 | tf_op jit(solution)/shard_map/psum | solution.py:165
  271.1 1.2 multiply_reduce_fusion
  272.9 1.2 multiply_divide_fusion
  274.1 0.9 copy.64
  (57 shorter events, 6.5 us)
Async XLA Ops:
  17.2 13.8 %all-to-all-start = ((s32[8,1,144]{2,1,0:T(1,128)}), s32[8,1,144]{2,1,0:T(1,128)S(1)}, u32[]{:S(2)}, u32[]{:S(2)}) async-start(s32[8,1,144]{2,1,0:T(1,128)} %all_to_all.12), calls=%async_computation | async-start | bytes 16384 | tf_op jit(solution)/shard_map/all_to_all | solution.py:119
  35.8 3.9 %copy-start.1 = (f32[256,200]{0,1:T(8,128)S(1)}, f32[256,200]{0,1:T(8,128)}, u32[]{:S(2)}) copy-start(f32[256,200]{0,1:T(8,128)} %param.9) | copy-start | bytes 614404
  35.8 4.0 %copy-start.3 = (s32[256]{0:T(256)S(1)}, s32[256]{0:T(256)}, u32[]{:S(2)}) copy-start(s32[256]{0:T(256)} %param.12) | copy-start | bytes 3076
  35.8 31.1 %all-to-all-start.1 = ((f32[8,144,200]{2,1,0:T(8,128)}), f32[8,144,200]{2,1,0:T(8,128)S(1)}, u32[]{:S(2)}, u32[]{:S(2)}) async-start(f32[8,144,200]{2,1,0:T(8,128)} %select_select_fusion), calls=%async_computation.1 | async-start | bytes 2359296 | tf_op jit(solution)/shard_map/all_to_all | solution.py:120
  84.0 145.0 %all-to-all-start.2 = ((f32[8,144,200]{2,1,0:T(8,128)}), f32[8,144,200]{2,1,0:T(8,128)S(1)}, u32[]{:S(2)}, u32[]{:S(2)}) async-start(f32[8,144,200]{2,1,0:T(8,128)} %bitcast.10), calls=%async_computation.2 | async-start | bytes 2359296 | tf_op jit(solution)/shard_map/all_to_all | solution.py:154
  87.6 140.9 %copy-start.4 = (f32[256]{0:T(256)S(1)}, f32[256]{0:T(256)}, u32[]{:S(2)}) copy-start(f32[256]{0:T(256)} %param.10) | copy-start | bytes 3076
  87.6 139.7 %all-reduce.5.cloned.1.call-start = ((), (), s32[]{:S(2)}) async-start(), calls=%async_computation.4 | async-start | bytes 524288 | tf_op jit(solution)/shard_map/psum | solution.py:162
  90.7 180.5 %all-reduce.3.cloned.1.call-start = ((), (), s32[]{:S(2)}) async-start(), calls=%async_computation.3 | async-start | bytes 1048576 | tf_op jit(solution)/shard_map/psum | solution.py:165
  227.3 11.1 %copy-start = (f32[256,200]{1,0:T(8,128)S(1)}, f32[256,200]{1,0:T(8,128)}, u32[]{:S(2)}) copy-start(f32[256,200]{1,0:T(8,128)} %all-reduce.5.cloned.1.call-done) | copy-start | bytes 614404
  229.0 43.3 %copy-start.2 = (f32[512]{0:T(512)S(1)}, f32[512]{0:T(512)}, u32[]{:S(2)}) copy-start(f32[512]{0:T(512)} %param.8) | copy-start | bytes 6148
Sparse Core Ops, SparseCore 0:
  94.5 132.8 all-reduce.4
Sparse Core Ops, SparseCore 1:
  238.5 32.6 all-reduce.2
where the time goes:
time: 284 us
  waiting for transfers between devices  152 us (54%)
  blocking collectives  45.4 us (16%)
  other arithmetic  23.6 us (8%)
  local copies, waits for them, and re-layouts  22.4 us (8%)
  between operations  18.9 us (7%)
  starting transfers between devices  15.1 us (5%)
  matrix products  5.94 us (2%)
    psum x1, waiting for transfers between devices, on_device(): lax.psum((relation_local, loss_local), ('ea', 'ba'))  89.3 us
    psum x1, blocking collectives, on_device(): lax.psum((relation_local, loss_local), ('ea', 'ba'))  45.4 us
    psum x1, waiting for transfers between devices, on_device(): summed = lax.psum(dense_grad, 'ba')  31.8 us
    all_to_all x1, waiting for transfers between devices, on_device(): lax.all_to_all(serve_rows(entities, joint_asked), 'ea', split_axis=0, con...  25.8 us
    scatter-add x1, other arithmetic, absorb(): dense_grad.at[flat_rows].add(incoming.reshape(-1, incoming.shape[-1]))  9.34 us
    all_to_all x1, starting transfers between devices, on_device(): lax.all_to_all(joint_request, 'ea', split_axis=0, concat_axis=0, tiled=True)  7.31 us
    scatter x1, local copies, waits for them, and re-layouts, outgoing_rows(): buffer_rows = jnp.zeros((peer_count * room_limit, slope_vector.shape[1]),...  6.55 us
  transfers between devices with their start and end apart: 5, of which 4 were waited for; matrix products, arithmetic and copies ran while one was open for 3% of the time, Pallas kernels for 0%

commit v1 on v0

--- a/solution.py
+++ b/solution.py
@@ -162,7 +162,8 @@
     relation_sum, loss_sum = lax.psum((relation_local, loss_local), ("ea", "ba"))
     relation_step, relation_squares = adagrad_step(relation_sum, relation_history)
     mean_loss = (loss_sum / (2.0 * edge_count * peer_count * lax.axis_size("ba"))).reshape(1)
-    summed = lax.psum(dense_grad, "ba")
+    parts = lax.all_gather(dense_grad, "ba", axis=0, tiled=False)
+    summed = parts.sum(axis=0)
     entity_step, entity_squares = adagrad_step(summed, entity_history)
     return (entity_step, entity_squares, relation_step, relation_squares, mean_loss)
 

time: 284 us -> 254 us (0.89)
  waiting for transfers between devices: 152 us -> 128 us
  blocking collectives: 45.4 us -> 38.5 us
    psum x1 -> x0, waiting for transfers between devices: 31.8 us -> none  [on_device(): summed = lax.psum(dense_grad, 'ba')]
    all_to_all x1, waiting for transfers between devices: 0.01 us -> 26.2 us  [on_device(): lax.all_to_all(outgoing_rows(joint_grad, joint_places, peer_count, joint_...]
    psum x1, waiting for transfers between devices: 89.3 us -> 71 us  [on_device(): lax.psum((relation_local, loss_local), ('ea', 'ba'))]
    psum x1, blocking collectives: 45.4 us -> 38.5 us  [on_device(): lax.psum((relation_local, loss_local), ('ea', 'ba'))]
  transfers between devices with their start and end apart: 5 -> 5, of which waited for: 4 -> 4; matrix products, arithmetic and copies ran while one was open for 3% -> 7% of each run, Pallas kernels for 0% -> 0%
where the time goes in v1:
time: 254 us
  waiting for transfers between devices  128 us (50%)
  blocking collectives  38.5 us (15%)
  other arithmetic  24.8 us (10%)
  local copies, waits for them, and re-layouts  22.1 us (9%)
  between operations  18.9 us (7%)
  starting transfers between devices  15.1 us (6%)
  matrix products  5.94 us (2%)
    psum x1, waiting for transfers between devices, on_device(): lax.psum((relation_local, loss_local), ('ea', 'ba'))  71 us
    psum x1, blocking collectives, on_device(): lax.psum((relation_local, loss_local), ('ea', 'ba'))  38.5 us
    all_to_all x1, waiting for transfers between devices, on_device(): lax.all_to_all(outgoing_rows(joint_grad, joint_places, peer_count, joint_...  26.2 us
    all_to_all x1, waiting for transfers between devices, on_device(): lax.all_to_all(serve_rows(entities, joint_asked), 'ea', split_axis=0, con...  25.8 us
    scatter-add x1, other arithmetic, absorb(): dense_grad.at[flat_rows].add(incoming.reshape(-1, incoming.shape[-1]))  9.33 us
    all_to_all x1, starting transfers between devices, on_device(): lax.all_to_all(joint_request, 'ea', split_axis=0, concat_axis=0, tiled=True)  7.31 us
    scatter x1, local copies, waits for them, and re-layouts, outgoing_rows(): buffer_rows = jnp.zeros((peer_count * room_limit, slope_vector.shape[1]),...  6.55 us
    all_to_all x1, waiting for transfers between devices, on_device(): lax.all_to_all(joint_request, 'ea', split_axis=0, concat_axis=0, tiled=True)  5.32 us
  transfers between devices with their start and end apart: 5, of which 4 were waited for; matrix products, arithmetic and copies ran while one was open for 7% of the time, Pallas kernels for 0%

profile of v1, /device:TPU:0, one launch (start us, length us, event | category | flops | bytes accessed | tf_op | source)
XLA Modules:
  0.0 253.7 jit_solution(14805222404088901553)
XLA Ops:
  8.0 0.8 fusion.40
  9.5 1.7 reduce-window.6
  11.7 0.7 multiply_subtract_fusion.6
  12.4 0.7 fusion.25
  13.2 3.4 %scatter_custom_fusion = s32[1152]{0:T(1024)S(1)} fusion(s32[768]{0:T(1024)S(1)} %fusion.25, s32[768]{0:T(1024)S(1)} %get-tuple-element.74, s32[]{:T(128)} %constant.34.clone.1), kind=kCustom, calls=%fused_computation.89 | custom fusion | bytes 4612 | tf_op jit(solution)/shard_map/scatter | solution.py:44
  17.2 7.3 %all-to-all-start = ((s32[8,1,144]{2,1,0:T(1,128)}), s32[8,1,144]{2,1,0:T(1,128)S(1)}, u32[]{:S(2)}, u32[]{:S(2)}) async-start(s32[8,1,144]{2,1,0:T(1,128)} %all_to_all.12), calls=%async_computation | async-start | bytes 16384 | tf_op jit(solution)/shard_map/all_to_all | solution.py:119
  24.5 1.2 copy.99
  25.8 5.3 %all-to-all-done = s32[8,1,144]{2,1,0:T(1,128)S(1)} async-done(((s32[8,1,144]{2,1,0:T(1,128)}), s32[8,1,144]{2,1,0:T(1,128)S(1)}, u32[]{:S(2)}, u32[]{:S(2)}) %all-to-all-start) | async-done | bytes 4640 | tf_op jit(solution)/shard_map/all_to_all | solution.py:119
  31.2 3.3 %gather_fusion = f32[1152,200]{1,0:T(8,128)S(1)} fusion(f32[512,200]{1,0:T(8,128)S(1)} %copy.99, s32[2048]{0:T(1024)S(1)} %pad_clamp_fusion), kind=kCustom, calls=%fused_computation | custom fusion | bytes 1847808 | tf_op jit(solution)/shard_map/jit(_take)/gather | solution.py:49
  34.5 1.3 select_select_fusion
  35.8 3.9 %all-to-all-start.1 = ((f32[8,144,200]{2,1,0:T(8,128)}), f32[8,144,200]{2,1,0:T(8,128)S(1)}, u32[]{:S(2)}, u32[]{:S(2)}) async-start(f32[8,144,200]{2,1,0:T(8,128)} %select_select_fusion), calls=%async_computation.1 | async-start | bytes 2359296 | tf_op jit(solution)/shard_map/all_to_all | solution.py:120
  39.9 1.0 gather_fusion.2
  41.0 25.8 %all-to-all-done.1 = f32[8,144,200]{2,1,0:T(8,128)S(1)} async-done(((f32[8,144,200]{2,1,0:T(8,128)}), f32[8,144,200]{2,1,0:T(8,128)S(1)}, u32[]{:S(2)}, u32[]{:S(2)}) %all-to-all-start.1) | async-done | bytes 921632 | tf_op jit(solution)/shard_map/all_to_all | solution.py:120
  66.9 2.1 gather_fusion.1
  69.8 1.2 fusion.43
  71.0 1.2 fusion.42
  73.1 1.1 fusion.8
  74.3 0.7 fusion.11
  75.0 0.7 fusion.14
  75.7 1.1 convolution_add_fusion
  77.4 6.6 %scatter_custom_fusion.1 = f32[1152,200]{1,0:T(8,128)} fusion(s32[768]{0:T(1024)S(1)} %fusion.25, f32[768,200]{1,0:T(8,128)S(1)} %copy.107, f32[]{:T(128)} %constant.33.clone.1), kind=kCustom, calls=%fused_computation.12 | custom fusion | bytes 921604 | tf_op jit(solution)/shard_map/scatter | solution.py:57
  84.0 3.6 %all-to-all-start.2 = ((f32[8,144,200]{2,1,0:T(8,128)}), f32[8,144,200]{2,1,0:T(8,128)S(1)}, u32[]{:S(2)}, u32[]{:S(2)}) async-start(f32[8,144,200]{2,1,0:T(8,128)} %bitcast.10), calls=%async_computation.2 | async-start | bytes 2359296 | tf_op jit(solution)/shard_map/all_to_all | solution.py:154
  88.0 2.6 %scatter_custom_fusion.3 = f32[256,200]{1,0:T(8,128)} fusion(s32[256]{0:T(256)S(1)} %copy-done.2, f32[256,200]{1,0:T(8,128)S(1)} %copy.110, f32[]{:T(128)} %constant.33.clone.1), kind=kCustom, calls=%fused_computation.40 | custom fusion | flops 51200 | bytes 204804 | tf_op jit(solution)/shard_map/scatter-add | solution.py:148
  90.7 26.2 %all-to-all-done.2 = f32[8,144,200]{2,1,0:T(8,128)S(1)} async-done(((f32[8,144,200]{2,1,0:T(8,128)}), f32[8,144,200]{2,1,0:T(8,128)S(1)}, u32[]{:S(2)}, u32[]{:S(2)}) %all-to-all-start.2) | async-done | bytes 921632 | tf_op jit(solution)/shard_map/all_to_all | solution.py:154
  116.9 9.3 %scatter_custom_fusion.2 = f32[512,200]{1,0:T(8,128)} fusion(s32[1152]{0:T(1024)S(1)} %reshape.425, f32[1152,200]{1,0:T(8,128)S(1)} %bitcast.46, f32[]{:T(128)} %constant.33.clone.1), kind=kCustom, calls=%fused_computation.29 | custom fusion | flops 230400 | bytes 409604 | tf_op jit(solution)/shard_map/scatter-add | solution.py:64
  127.5 38.5 %psum.15 = f32[]{:T(128)} all-reduce(f32[]{:T(128)S(6)} %add.181), channel_id=1, replica_groups=mesh['ea'=8,'ba'=4] {'ea','ba'}, use_global_device_ids=true, to_apply=%region_18.19 | all-reduce | flops 1 | bytes 8 | tf_op jit(solution)/shard_map/psum | solution.py:162
  166.7 71.0 %all-reduce.2.cloned.1.call-done = f32[256,200]{1,0:T(8,128)} async-done(((f32[256,200]{1,0:T(8,128)}), f32[256,200]{1,0:T(8,128)}) %all-reduce.2.cloned.1.call-update) | async-done | bytes 204816 | tf_op jit(solution)/shard_map/psum | solution.py:162
  237.7 1.1 multiply_reduce_fusion.1
  239.3 1.1 multiply_divide_fusion.1
  240.4 0.8 copy.111
  241.2 1.8 reduce_sum.88
  244.3 0.8 multiply_divide_fusion
  (56 shorter events, 7.1 us)
Async XLA Ops:
  17.2 13.8 %all-to-all-start = ((s32[8,1,144]{2,1,0:T(1,128)}), s32[8,1,144]{2,1,0:T(1,128)S(1)}, u32[]{:S(2)}, u32[]{:S(2)}) async-start(s32[8,1,144]{2,1,0:T(1,128)} %all_to_all.12), calls=%async_computation | async-start | bytes 16384 | tf_op jit(solution)/shard_map/all_to_all | solution.py:119
  35.8 3.9 %copy-start = (f32[256,200]{0,1:T(8,128)S(1)}, f32[256,200]{0,1:T(8,128)}, u32[]{:S(2)}) copy-start(f32[256,200]{0,1:T(8,128)} %param.9) | copy-start | bytes 614404
  35.8 4.0 %copy-start.2 = (s32[256]{0:T(256)S(1)}, s32[256]{0:T(256)}, u32[]{:S(2)}) copy-start(s32[256]{0:T(256)} %param.12) | copy-start | bytes 3076
  35.8 31.1 %all-to-all-start.1 = ((f32[8,144,200]{2,1,0:T(8,128)}), f32[8,144,200]{2,1,0:T(8,128)S(1)}, u32[]{:S(2)}, u32[]{:S(2)}) async-start(f32[8,144,200]{2,1,0:T(8,128)} %select_select_fusion), calls=%async_computation.1 | async-start | bytes 2359296 | tf_op jit(solution)/shard_map/all_to_all | solution.py:120
  84.0 32.9 %all-to-all-start.2 = ((f32[8,144,200]{2,1,0:T(8,128)}), f32[8,144,200]{2,1,0:T(8,128)S(1)}, u32[]{:S(2)}, u32[]{:S(2)}) async-start(f32[8,144,200]{2,1,0:T(8,128)} %bitcast.10), calls=%async_computation.2 | async-start | bytes 2359296 | tf_op jit(solution)/shard_map/all_to_all | solution.py:154
  87.6 150.1 %all-reduce.2.cloned.1.call-start = ((), (), s32[]{:S(2)}) async-start(), calls=%async_computation.3 | async-start | bytes 524288 | tf_op jit(solution)/shard_map/psum | solution.py:162
  87.9 150.9 %copy-start.3 = (f32[256]{0:T(256)S(1)}, f32[256]{0:T(256)}, u32[]{:S(2)}) copy-start(f32[256]{0:T(256)} %param.10) | copy-start | bytes 3076
  90.7 150.5 %all-gather.3.cloned.1.call-start = ((), (), s32[]{:S(2)}) async-start(), calls=%async_computation.4 | async-start | bytes 2621440 | tf_op jit(solution)/shard_map/all_gather | solution.py:165
  243.0 0.7 copy-start.1
Sparse Core Ops, SparseCore 0:
  94.4 143.2 all-reduce.1
Sparse Core Ops, SparseCore 1:
  126.3 21.8 all-gather.2
